TPU v7x, 256 devices: a whole 4x4x8 slice. The times are simulated.
256 devices in a mesh: robot: 64 (over x, z, core), sub: 4 (over y).
Axes of the slice: x: 4, y: 4, z: 8, core: 2. Of those that a mesh axis runs over, the one named last changes fastest.
Arguments:
- landmark_copies: float32 [64, 4, 3, 4096], P('robot', 'sub'), may hold values from -6 to 6
- dual_copies: float32 [64, 4, 3, 4096], P('robot', 'sub'), may hold values from -4 to 4
- visibility: int32 [64, 4, 4096], P('robot', 'sub'), may hold values from 0 to 511
- block_counts: int32 [64, 4, 64], P('robot', 'sub'), may hold values from 1 to 64, as said below
- consensus_old: float32 [64, 4, 3, 512], P('robot', 'sub'), may hold values from -6 to 6
- poses: float32 [64, 4, 6, 1024], P('robot', 'sub'), may hold values from -6 to 6
- inverse_blocks: float32 [64, 4, 36, 1024], P('robot', 'sub'), may hold values from -1.8 to 1.8
- jacobians: float32 [64, 4, 18, 4096], P('robot', 'sub'), may hold values from -3 to 3
- measurements: float32 [64, 4, 3, 4096], P('robot', 'sub'), may hold values from -6 to 6
- obs_pose: int32 [64, 4, 4096], P('robot', 'sub'), may hold values from 0 to 1023
- obs_slot: int32 [64, 4, 4096], P('robot', 'sub'), may hold values from 0 to 4095, as said below
- edge_to: int32 [64, 4, 1024], P('robot', 'sub'), may hold values from 0 to 4095
- edge_offset: float32 [64, 4, 6, 1024], P('robot', 'sub'), may hold values from -3 to 3
Outputs:
- refined_poses: float32 [64, 4, 6, 1024], P('robot', 'sub')
- consensus: float32 [64, 4, 3, 512], P('robot', 'sub')
- dual_new: float32 [64, 4, 3, 4096], P('robot', 'sub')
- residual_norms: float32 [2], replicated
Inputs may be any that keep to these rules, and one draw needn't show every extreme that they name: block_counts[r,s,d] counts the live slots at the head of block d; for every sub index some robot receives full blocks from every robot, which robot varies with the draw. `obs_slot`: each observation names a live slot of its own device.
All inputs are finite; a program needn't handle non-finite values.
Results may differ from a plain program's by a relative error of at most 0.0001.
Values sent between devices are 32-bit elements; how exact they have to be, the bound alone decides.
A program may use at most 64 MiB of HBM per device.

v0:
```python
import jax
import jax.numpy as jnp
from jax import lax
from jax.sharding import Mesh
from jax.sharding import PartitionSpec as P

ROBOT = ("robot_0", "robot_1", "robot_2")
ROBOT_SUB = ("robot_0", "robot_1", "robot_2", "sub")


penalty = 2.0


def over_axes(x, axes):
    for axis in axes:
        x = lax.psum(x, axis)
    return x


def copy_for_each(x, axis):
    length = lax.axis_size(axis)
    return lax.all_to_all(jnp.broadcast_to(x[None], (length, *x.shape)), axis, 0, 0, tiled=True)


def laid_out(pieces, dim):
    dims = list(pieces.shape[1:])
    dims[dim] *= pieces.shape[0]
    return jnp.moveaxis(pieces, 0, dim).reshape(dims)


def collect(x, axis, dim):
    pieces = copy_for_each(x, axis)
    return laid_out(pieces, dim)


def body(
    landmark_copies,
    dual_copies,
    visibility,
    block_counts,
    consensus_old,
    poses,
    inverse_blocks,
    jacobians,
    measurements,
    obs_pose,
    obs_slot,
    edge_to,
    edge_offset,
):
    copies = landmark_copies[0, 0]
    duals = dual_copies[0, 0]
    slot_ids = visibility[0]
    counts = block_counts[0, 0]
    old_estimate = consensus_old[0, 0]
    robots = lax.axis_size(ROBOT)
    slot_count = copies.shape[1]
    block_size = slot_count // robots
    owned = old_estimate.shape[1]
    live_mask = (
        (jnp.arange(block_size)[None, :] < counts[:, None]).reshape(slot_count).astype(jnp.float32)
    )
    outgoing = jnp.concatenate([(copies + duals) * live_mask[None, :], live_mask[None, :]], axis=0)
    received, received_ids = (
        lax.all_to_all(outgoing, ROBOT, split_axis=1, concat_axis=1, tiled=True),
        lax.all_to_all(slot_ids, ROBOT, split_axis=1, concat_axis=1, tiled=True),
    )
    owner_ids = received_ids[0]
    totals = jax.vmap(lambda entries: jax.ops.segment_sum(entries, owner_ids, num_segments=owned))(
        received
    )
    consensus = (old_estimate + totals[:3]) / (1.0 + totals[3:4])
    returning = consensus[:, owner_ids]
    back = lax.all_to_all(returning, ROBOT, split_axis=1, concat_axis=1, tiled=True)
    differ = (copies - back) * live_mask[None, :]
    dual_new = duals + differ
    primal = jnp.sum(differ * differ)
    change = consensus - old_estimate
    dualsum = penalty * penalty * jnp.sum(totals[3:4] * change * change)
    primal_all, dual_all = (over_axes(primal, ROBOT_SUB), over_axes(dualsum, ROBOT_SUB))
    landmark_total = owned * robots * lax.axis_size("sub")
    residual_norms = jnp.sqrt(jnp.stack([primal_all, dual_all]) / landmark_total)
    pose_block = poses[0, 0]
    pose_count = pose_block.shape[1]
    robot_all = collect(pose_block, "sub", 1)
    pose_far = robot_all[:, edge_to[0, 0]]
    copies_at = copies[:, obs_slot[0, 0]]
    error = measurements[0, 0] - copies_at
    jac_rows = jacobians[0, 0].reshape(3, 6, error.shape[1])
    pull = jnp.sum(jac_rows * error[:, None, :], axis=0)
    pose_ids = obs_pose[0, 0]
    grad_obs = jax.vmap(
        lambda entries: jax.ops.segment_sum(entries, pose_ids, num_segments=pose_count)
    )(pull)
    grad = grad_obs + pose_far - pose_block - edge_offset[0, 0]
    inverse = inverse_blocks[0, 0].reshape(6, 6, pose_count)
    delta = jnp.sum(inverse * grad[None, :, :], axis=1)
    refined = pose_block + delta
    return (refined[None, None], consensus[None, None], dual_new[None, None], residual_norms)


def solution(mesh):
    finer = Mesh(
        mesh.devices.reshape(4, 8, 2, mesh.shape["sub"]), ("robot_0", "robot_1", "robot_2", "sub")
    )
    return jax.shard_map(
        body,
        mesh=finer,
        in_specs=(
            P(ROBOT, "sub", None, None),
            P(ROBOT, "sub", None, None),
            P(ROBOT, "sub", None),
            P(ROBOT, "sub", None),
            P(ROBOT, "sub", None, None),
            P(ROBOT, "sub", None, None),
            P(ROBOT, "sub", None, None),
            P(ROBOT, "sub", None, None),
            P(ROBOT, "sub", None, None),
            P(ROBOT, "sub", None),
            P(ROBOT, "sub", None),
            P(ROBOT, "sub", None),
            P(ROBOT, "sub", None, None),
        ),
        out_specs=(
            P(ROBOT, "sub", None, None),
            P(ROBOT, "sub", None, None),
            P(ROBOT, "sub", None, None),
            P(),
        ),
        check_vma=False,
    )
```

profile of v0, /device:TPU:1, one launch (start us, length us, event | category | flops | bytes accessed | tf_op | source)
XLA Modules:
  0.0 213.6 jit_solution(6350417667022919930)
XLA Ops:
  0.7 0.5 broadcast.121
  1.2 1.4 reduce.16
  2.6 0.7 all_to_all.26
  3.3 13.0 %all-to-all-start.1 = ((s32[1,64,64]{2,0,1:T(1,128)}), s32[1,64,64]{2,0,1:T(1,128)S(1)}, u32[]{:S(2)}, u32[]{:S(2)}) async-start(s32[1,64,64]{2,0,1:T(1,128)} %all_to_all.26), calls=%async_computation.1 | async-start | bytes 65536 | tf_op jit(solution)/shard_map/all_to_all | solution.py:66
  16.3 0.7 fusion.8
  17.0 0.7 fusion.9
  17.7 1.4 copy.54
  19.2 0.2 add_reduce_fusion.1
  19.3 0.1 add.91
  19.5 2.0 copy.53
  21.5 14.1 %gather_fusion.1 = f32[4096,3]{1,0:T(8,128)} fusion(f32[3,4096]{0,1:T(8,128)S(1)} %bitcast.57, s32[4096]{0:T(1024)S(1)} %broadcast_clamp_fusion.1), kind=kCustom, calls=%fused_computation.1 | custom fusion | bytes 114688 | tf_op jit(solution)/shard_map/gather | solution.py:87
  35.6 3.7 %bitcast_subtract_fusion.1 = f32[3,4096]{0,1:T(8,128)} fusion(f32[4096,3]{1,0:T(8,128)} %gather_fusion.1, f32[1,1,3,4096]{2,3,1,0:T(8,128)} %copy.53), kind=kLoop, calls=%fused_computation.9 | loop fusion | flops 12288 | bytes 147456 | tf_op jit(solution)/shard_map/sub | solution.py:88
  39.3 2.3 %copy.55 = f32[3,4096]{1,0:T(4,128)S(1)} copy(f32[3,4096]{0,1:T(8,128)} %bitcast_subtract_fusion.1) | data formatting | bytes 98304 | tf_op jit(solution)/shard_map/sub | solution.py:88
  41.6 0.7 reduce.1
  42.5 0.7 reshape.197
  43.2 0.2 copy.50
  43.4 0.1 copy.82
  43.5 0.8 reshape.266
  44.3 0.8 copy.59
  45.1 2.0 copy.56
  47.1 1.0 copy.57
  48.1 1.3 reduce
  49.4 0.7 reshape_squeeze.6
  50.1 0.7 broadcast_in_dim.9
  50.8 4.2 %all-to-all-start = ((f32[4,6,1024]{2,1,0:T(8,128)}), f32[4,6,1024]{2,1,0:T(8,128)S(1)}, u32[]{:S(2)}, u32[]{:S(2)}) async-start(f32[4,6,1024]{2,1,0:T(8,128)} %broadcast_in_dim.9), calls=%async_computation | async-start | bytes 262144 | tf_op jit(solution)/shard_map/all_to_all | solution.py:22
  54.9 0.1 broadcast_in_dim_squeeze.9
  55.1 0.6 broadcast_clamp_fusion
  55.7 0.7 reduce.17
  56.4 0.7 reshape.232
  57.1 2.7 %all-to-all-done = f32[4,6,1024]{2,1,0:T(8,128)S(1)} async-done(((f32[4,6,1024]{2,1,0:T(8,128)}), f32[4,6,1024]{2,1,0:T(8,128)S(1)}, u32[]{:S(2)}, u32[]{:S(2)}) %all-to-all-start) | async-done | bytes 98336 | tf_op jit(solution)/shard_map/all_to_all | solution.py:22
  59.8 11.8 %all-to-all-start.2 = ((f32[64,1,256]{2,1,0:T(1,128)}), f32[64,1,256]{2,1,0:T(1,128)S(1)}, u32[]{:S(2)}, u32[]{:S(2)}) async-start(f32[64,1,256]{2,1,0:T(1,128)} %reshape.266), calls=%async_computation.2 | async-start | bytes 131072 | tf_op jit(solution)/shard_map/all_to_all | solution.py:65
  71.5 1.9 copy.52
  73.5 4.4 %gather_fusion = f32[1024,6]{1,0:T(8,128)S(1)} fusion(f32[6,4096]{0,1:T(8,128)} %bitcast.60, s32[1024]{0:T(1024)S(1)} %broadcast_clamp_fusion.2), kind=kCustom, calls=%fused_computation | custom fusion | bytes 53248 | tf_op jit(solution)/shard_map/gather | solution.py:86
  77.9 22.9 %scatter_fusion = f32[6,1024]{0,1:T(8,128)S(1)} fusion(f32[6,1024]{0,1:T(8,128)S(1)} %bitcast.58, s32[4096]{0:T(1024)} %bitcast.74, f32[4096,6]{1,0:T(8,128)} %copy.56), kind=kCustom, calls=%fused_computation.3 | custom fusion | flops 24576 | bytes 311296 | tf_op jit(solution)/shard_map/vmap()/scatter-add | solution.py:93
  100.7 1.9 bitcast_subtract_fusion.2
  102.7 1.2 copy.58
  103.9 1.0 multiply_reduce_fusion.1
  104.9 0.5 broadcast.123
  105.4 0.8 reduce.18
  106.2 0.1 reshape.267
  106.4 0.1 reshape.231
  106.5 2.0 copy.62
  108.5 22.9 %scatter_custom_fusion.1 = f32[4,512]{0,1:T(8,128)S(1)} fusion(s32[4096]{0:T(1024)} %reshape.232, f32[4096,4]{1,0:T(8,128)} %copy.62, f32[]{:T(128)} %constant.9.clone.1), kind=kCustom, calls=%fused_computation.22 | custom fusion | flops 16384 | bytes 8704 | tf_op jit(solution)/shard_map/vmap()/scatter-add | solution.py:69
  131.4 0.3 slice_reduce_fusion
  131.7 0.8 fusion.3
  132.5 14.1 %gather_fusion.2 = f32[4096,3]{1,0:T(8,128)} fusion(f32[3,512]{0,1:T(8,128)S(1)} %get-tuple-element.31, s32[4096]{0:T(1024)S(1)} %copy-done.6), kind=kCustom, calls=%fused_computation.2 | custom fusion | bytes 114688 | tf_op jit(solution)/shard_map/gather | solution.py:73
  146.6 2.3 %copy.63 = f32[3,64,64]{2,0,1:T(4,128)S(1)} copy(f32[3,64,64]{0,2,1:T(8,128)} %bitcast.61) | data formatting | bytes 98304 | tf_op jit(solution)/shard_map/all_to_all | solution.py:74
  148.9 0.8 reshape.268
  149.6 10.3 %all-to-all-start.3 = ((f32[64,1,192]{2,1,0:T(1,128)}), f32[64,1,192]{2,1,0:T(1,128)S(1)}, u32[]{:S(2)}, u32[]{:S(2)}) async-start(f32[64,1,192]{2,1,0:T(1,128)} %reshape.268), calls=%async_computation.3 | async-start | bytes 131072 | tf_op jit(solution)/shard_map/all_to_all | solution.py:74
  159.9 0.6 reshape_add_fusion
  160.6 0.7 copy.68
  161.9 7.8 %all-to-all-done.3 = f32[64,1,192]{2,1,0:T(1,128)S(1)} async-done(((f32[64,1,192]{2,1,0:T(1,128)}), f32[64,1,192]{2,1,0:T(1,128)S(1)}, u32[]{:S(2)}, u32[]{:S(2)}) %all-to-all-start.3) | async-done | bytes 49184 | tf_op jit(solution)/shard_map/all_to_all | solution.py:74
  169.7 0.8 reduce.19
  170.5 0.1 reshape.269
  170.6 2.0 copy.67
  172.7 0.1 all_to_all.32
  172.8 2.5 %fusion.2 = f32[]{:T(128)} fusion(f32[3,64,64]{0,2,1:T(8,128)} %copy.67, f32[4096]{0:T(1024)S(1)} %copy-done.5, f32[1,1,3,4096]{2,3,1,0:T(8,128)S(1)} %copy.54), kind=kLoop, calls=%fused_computation.8 | loop fusion | flops 49151 | bytes 114692 | tf_op jit(solution)/shard_map/reduce_sum | solution.py:77
  175.4 0.1 copy_add_fusion
  175.4 0.7 copy.69
  176.1 7.4 %all-reduce.2 = (f32[]{:T(128)}, f32[]{:T(128)}) all-reduce(f32[]{:T(128)S(6)} %mul_shard_map.3, f32[]{:T(128)} %fusion.2), channel_id=1, replica_groups=mesh['robot_0'=4,'robot_1'=8,'robot_2'=2,'sub'=4] {'robot_0'}, use_global_device_ids=true, to_apply=%region_10.0 | all-reduce | flops 2 | bytes 16 | tf_op jit(solution)/shard_map/psum | solution.py:16
  183.5 11.8 %all-reduce = (f32[]{:T(128)}, f32[]{:T(128)}) all-reduce(f32[]{:T(128)} %get-tuple-element.26, f32[]{:T(128)} %get-tuple-element.27), channel_id=1, replica_groups=mesh['robot_0'=4,'robot_1'=8,'robot_2'=2,'sub'=4] {'robot_1'}, use_global_device_ids=true, to_apply=%region_11.0 | all-reduce | flops 2 | bytes 16 | tf_op jit(solution)/shard_map/psum | solution.py:16
  195.3 9.0 %all-reduce.3 = (f32[]{:T(128)}, f32[]{:T(128)}) all-reduce(f32[]{:T(128)} %get-tuple-element.22, f32[]{:T(128)} %get-tuple-element.23), channel_id=1, replica_groups=mesh['robot_0'=4,'robot_1'=8,'robot_2'=2,'sub'=4] {'robot_2'}, use_global_device_ids=true, to_apply=%region_12.0 | all-reduce | flops 2 | bytes 16 | tf_op jit(solution)/shard_map/psum | solution.py:16
  204.3 7.5 %all-reduce.1 = (f32[1]{0:T(128)}, f32[1]{0:T(128)}) all-reduce(f32[1]{0:T(128)} %bitcast.24, f32[1]{0:T(128)} %bitcast.23), channel_id=1, replica_groups=mesh['robot_0'=4,'robot_1'=8,'robot_2'=2,'sub'=4] {'sub'}, use_global_device_ids=true, to_apply=%region_13.0 | all-reduce | flops 2 | bytes 16 | tf_op jit(solution)/shard_map/psum | solution.py:16
  211.8 1.8 fusion.10
  (36 shorter events, 0.3 us)
Async XLA Ops:
  0.6 18.5 %copy-start = (f32[1,1,3,4096]{3,1,2,0:T(1,128)S(1)}, f32[1,1,3,4096]{3,1,2,0:T(1,128)}, u32[]{:S(2)}) copy-start(f32[1,1,3,4096]{3,1,2,0:T(1,128)} %param.13) | copy-start | bytes 147460
  0.6 18.5 %copy-start.3 = (f32[1,1,3,4096]{3,1,2,0:T(1,128)S(1)}, f32[1,1,3,4096]{3,1,2,0:T(1,128)}, u32[]{:S(2)}) copy-start(f32[1,1,3,4096]{3,1,2,0:T(1,128)} %param.14) | copy-start | bytes 147460
  0.7 18.8 %copy-start.9 = (s32[1,1,4096]{2,1,0:T(1,128)S(1)}, s32[1,1,4096]{2,1,0:T(1,128)}, u32[]{:S(2)}) copy-start(s32[1,1,4096]{2,1,0:T(1,128)} %param.23) | copy-start | bytes 49156
  0.7 18.8 %copy-start.7 = (f32[1,1,3,4096]{3,1,2,0:T(1,128)S(1)}, f32[1,1,3,4096]{3,1,2,0:T(1,128)}, u32[]{:S(2)}) copy-start(f32[1,1,3,4096]{3,1,2,0:T(1,128)} %param.21) | copy-start | bytes 147460
  3.3 46.8 %all-to-all-start.1 = ((s32[1,64,64]{2,0,1:T(1,128)}), s32[1,64,64]{2,0,1:T(1,128)S(1)}, u32[]{:S(2)}, u32[]{:S(2)}) async-start(s32[1,64,64]{2,0,1:T(1,128)} %all_to_all.26), calls=%async_computation.1 | async-start | bytes 65536 | tf_op jit(solution)/shard_map/all_to_all | solution.py:66
  39.3 2.3 %copy-start.1 = (f32[1,1,18,4096]{3,1,2,0:T(1,128)S(1)}, f32[1,1,18,4096]{3,1,2,0:T(1,128)}, u32[]{:S(2)}) copy-start(f32[1,1,18,4096]{3,1,2,0:T(1,128)} %param.20) | copy-start | bytes 884740
  39.3 3.0 %copy-start.10 = (s32[1,1,1024]{2,1,0:T(1,128)S(1)}, s32[1,1,1024]{2,1,0:T(1,128)}, u32[]{:S(2)}) copy-start(s32[1,1,1024]{2,1,0:T(1,128)} %param.24) | copy-start | bytes 12292
  39.3 3.9 %copy-start.2 = (f32[1,1,6,1024]{3,1,2,0:T(1,128)S(1)}, f32[1,1,6,1024]{3,1,2,0:T(1,128)}, u32[]{:S(2)}) copy-start(f32[1,1,6,1024]{3,1,2,0:T(1,128)} %param.18) | copy-start | bytes 73732
  42.5 4.6 %copy-start.8 = (f32[1,1,6,1024]{3,1,2,0:T(1,128)S(1)}, f32[1,1,6,1024]{3,1,2,0:T(1,128)}, u32[]{:S(2)}) copy-start(f32[1,1,6,1024]{3,1,2,0:T(1,128)} %param.25) | copy-start | bytes 73732
  50.8 9.0 %all-to-all-start = ((f32[4,6,1024]{2,1,0:T(8,128)}), f32[4,6,1024]{2,1,0:T(8,128)S(1)}, u32[]{:S(2)}, u32[]{:S(2)}) async-start(f32[4,6,1024]{2,1,0:T(8,128)} %broadcast_in_dim.9), calls=%async_computation | async-start | bytes 262144 | tf_op jit(solution)/shard_map/all_to_all | solution.py:22
  59.8 45.1 %all-to-all-start.2 = ((f32[64,1,256]{2,1,0:T(1,128)}), f32[64,1,256]{2,1,0:T(1,128)S(1)}, u32[]{:S(2)}, u32[]{:S(2)}) async-start(f32[64,1,256]{2,1,0:T(1,128)} %reshape.266), calls=%async_computation.2 | async-start | bytes 131072 | tf_op jit(solution)/shard_map/all_to_all | solution.py:65
  106.2 26.3 %copy-start.6 = (s32[4096]{0:T(1024)S(1)}, s32[4096]{0:T(1024)}, u32[]{:S(2)}) copy-start(s32[4096]{0:T(1024)} %broadcast_clamp_fusion) | copy-start | bytes 49156
  148.9 23.9 %copy-start.5 = (f32[4096]{0:T(1024)S(1)}, f32[4096]{0:T(1024)}, u32[]{:S(2)}) copy-start(f32[4096]{0:T(1024)} %reshape.197) | copy-start | bytes 49156
  149.6 20.1 %all-to-all-start.3 = ((f32[64,1,192]{2,1,0:T(1,128)}), f32[64,1,192]{2,1,0:T(1,128)S(1)}, u32[]{:S(2)}, u32[]{:S(2)}) async-start(f32[64,1,192]{2,1,0:T(1,128)} %reshape.268), calls=%async_computation.3 | async-start | bytes 131072 | tf_op jit(solution)/shard_map/all_to_all | solution.py:74
  172.8 2.6 %copy-start.4 = (f32[1,1,3,4096]{3,1,2,0:T(1,128)S(1)}, f32[1,1,3,4096]{3,1,2,0:T(1,128)}, u32[]{:S(2)}) copy-start(f32[1,1,3,4096]{3,1,2,0:T(1,128)} %param.14) | copy-start | bytes 147460
where the time goes:
time: 215 us; the launch traced here: 214 us
  other arithmetic  66.6 us (31%)
  local copies, waits for them, and re-layouts  59.9 us (28%)
  starting transfers between devices  39.2 us (18%)
  blocking collectives  35.7 us (17%)
  waiting for transfers between devices  10.5 us (5%)
    psum x4, blocking collectives, over_axes(): x = lax.psum(x, axis)  35.7 us
    scatter-add x1, other arithmetic, body(): jax.ops.segment_sum(entries, owner_ids, num_segments=owned)  22.9 us
    scatter-add x1, other arithmetic, body(): jax.ops.segment_sum(entries, pose_ids, num_segments=pose_count)  22.9 us
    gather x1, local copies, waits for them, and re-layouts, body(): copies_at = copies[:, obs_slot[0, 0]]  14.1 us
    gather x1, local copies, waits for them, and re-layouts, body(): returning = consensus[:, owner_ids]  14.1 us
    all_to_all x1, starting transfers between devices, body(): lax.all_to_all(slot_ids, ROBOT, split_axis=1, concat_axis=1, tiled=True)  13 us
    all_to_all x1, starting transfers between devices, body(): lax.all_to_all(outgoing, ROBOT, split_axis=1, concat_axis=1, tiled=True)  11.8 us
    all_to_all x1, starting transfers between devices, body(): lax.all_to_all(returning, ROBOT, split_axis=1, concat_axis=1, tiled=True)  10.3 us
  transfers between devices with their start and end apart: 4, of which 2 were waited for; matrix products, arithmetic and copies ran while one was open for 33% of the time, Pallas kernels for 0%

commit v1 on v0

v1 whole, which is shorter than its diff:
```python
import functools

import jax
import jax.numpy as jnp
from jax import lax
from jax.experimental import pallas as pl
from jax.experimental.pallas import tpu as pltpu
from jax.sharding import PartitionSpec as P

MESH = pl.DeviceIdType.MESH
NX, NZ, SUBS = 4, 8, 4
CHIPS = NX * NZ
LANES = 128
PENALTY = 2.0
LANDMARKS = 131072.0
F32, BF16, I32 = jnp.float32, jnp.bfloat16, jnp.int32

OFFSETS = sorted(
    ((dx, dz) for dx in range(NX) for dz in range(NZ)),
    key=lambda o: (min(o[0], NX - o[0]) + min(o[1], NZ - o[1]), o),
)


def lane_gather(row, index):
    return jnp.take_along_axis(
        jnp.broadcast_to(row, index.shape), index, axis=1, mode="promise_in_bounds"
    )


def three_parts(x):
    high = x.astype(BF16).astype(F32)
    rest = x - high
    middle = rest.astype(BF16).astype(F32)
    return [high, middle, rest - middle]


def one_hot(lo_row):
    rows = lax.broadcasted_iota(I32, (LANES, LANES), 0)
    return jnp.where(rows == lo_row, 1.0, 0.0).astype(BF16)


def dot_entries(a, b):
    return lax.dot_general(a, b, (((1,), (1,)), ((), ())), preferred_element_type=F32)


def kernel(
    lc_h, dc_h, vis_h, cnt_h, cold_h, pose_h, inv_h, jac_h, meas_h, opose_h, oslot_h, edge_h, eoff_h,
    refined_h, cons_h, dual_h, norms_ref,
    lc, dc, vis, cnt, cold, pose, inv, jac, meas, opose, oslot, edge, eoff,
    send, recv, pull, totals, other_totals, other_cold, all_poses, returning, back, part, part1, part2,
    refined, cons, dual,
    load_sem, send_sem, recv_sem, y_send, y_recv, d2d_send, d2d_recv, ret_send, ret_recv,
    p1_send, p1_recv, p2_send, p2_recv, out_sem,
):
    robot, sub = lax.axis_index("robot"), lax.axis_index("sub")
    core, chip = lax.rem(robot, 2), lax.div(robot, 2)
    x, z = lax.div(chip, NZ), lax.rem(chip, NZ)

    loads = [
        pltpu.make_async_copy(src, dst, load_sem.at[i])
        for i, (src, dst) in enumerate(
            [(lc_h, lc), (dc_h, dc), (vis_h, vis), (cnt_h, cnt), (pose_h, pose), (cold_h, cold), (oslot_h, oslot),
             (meas_h, meas), (jac_h, jac), (opose_h, opose), (edge_h, edge), (eoff_h, eoff), (inv_h, inv)]
        )
    ]
    for load in loads:
        load.start()

    def at_offset(k, sign=1):
        dx, dz = OFFSETS[k]
        px = lax.rem(x + (dx if sign > 0 else NX - dx), NX)
        pz = lax.rem(z + (dz if sign > 0 else NZ - dz), NZ)
        return px * NZ + pz

    group = [(dc_, ds) for dc_ in range(2) for ds in range(SUBS) if (dc_, ds) != (0, 0)]

    def group_peer(dc_, ds):
        return {
            "robot": chip * 2 + lax.rem(core + dc_, 2),
            "sub": lax.rem(sub + ds, SUBS),
        }

    barrier = pltpu.get_barrier_semaphore()
    for k in range(1, CHIPS):
        pl.semaphore_signal(
            barrier,
            inc=1,
            device_id={"robot": at_offset(k) * 2 + core, "sub": sub},
            device_id_type=MESH,
        )
    for dc_, ds in group:
        pl.semaphore_signal(
            barrier, inc=1, device_id=group_peer(dc_, ds), device_id_type=MESH
        )

    for i in range(4):
        loads[i].wait()
    lane = lax.broadcasted_iota(I32, (CHIPS, LANES), 1)
    counts = jnp.broadcast_to(cnt[...].astype(F32), (CHIPS, 64))
    at = lax.broadcasted_iota(I32, (CHIPS, 64), 1)
    row2 = lax.broadcasted_iota(I32, (CHIPS, 64), 0) * 2
    even = jnp.sum(jnp.where(at == row2, counts, 0.0), axis=1, keepdims=True)
    odd = jnp.sum(jnp.where(at == row2 + 1, counts, 0.0), axis=1, keepdims=True)
    limit = jnp.where(lane < 64, even, odd)
    live = jnp.where((lane & 63).astype(F32) < limit, 1.0, 0.0)
    for v in range(3):
        send[:, v, :] = lc[v]
        send[:, 3 + v, :] = (lc[v] + dc[v]) * live
    send[:, 6, :] = live
    send[:, 7, :] = vis[...].astype(F32)
    recv[0] = send[chip]
    loads[4].wait()
    all_poses[sub] = pose[...]
    loads[5].wait()

    pl.semaphore_wait(barrier, CHIPS - 1 + len(group))

    def exchange(k):
        peer = at_offset(k)
        return pltpu.make_async_remote_copy(
            src_ref=send.at[peer],
            dst_ref=recv.at[k],
            send_sem=send_sem,
            recv_sem=recv_sem.at[k],
            device_id={"robot": peer * 2 + core, "sub": sub},
            device_id_type=MESH,
        )

    for k in range(CHIPS - 1, 0, -1):
        exchange(k).start()
    y_copies = [
        pltpu.make_async_remote_copy(
            src_ref=pose,
            dst_ref=all_poses.at[sub],
            send_sem=y_send.at[ds - 1],
            recv_sem=y_recv.at[ds - 1],
            device_id={"robot": robot, "sub": lax.rem(sub + ds, SUBS)},
            device_id_type=MESH,
        )
        for ds in range(1, SUBS)
    ]
    for copy in y_copies:
        copy.start()
    partner = group_peer(1, 0)
    cold_copy = pltpu.make_async_remote_copy(
        src_ref=cold,
        dst_ref=other_cold,
        send_sem=d2d_send.at[0],
        recv_sem=d2d_recv.at[0],
        device_id=partner,
        device_id_type=MESH,
    )
    cold_copy.start()

    loads[6].wait()
    blocks = [slice(8 * b, 8 * b + 8) for b in range(4)]
    slot_lo = [oslot[b, :] & 127 for b in blocks]
    slot_hi = [oslot[b, :] >> 7 for b in blocks]

    def gather_copies(h, found):
        new = []
        for v in range(3):
            row = lc[v, pl.ds(h, 1), :]
            for b in range(4):
                new.append(jnp.where(slot_hi[b] == h, lane_gather(row, slot_lo[b]), found[4 * v + b]))
        return tuple(new)

    zero = jnp.zeros((8, LANES), F32)
    found = lax.fori_loop(0, 32, gather_copies, (zero,) * 12, unroll=4)
    for i in (7, 8, 9):
        loads[i].wait()
    for b in range(4):
        error = [meas[v, blocks[b], :] - found[4 * v + b] for v in range(3)]
        for a in range(6):
            pull[a, blocks[b], :] = sum(jac[6 * k + a, blocks[b], :] * error[k] for k in range(3))

    sub8 = lax.broadcasted_iota(I32, (8, LANES), 0)

    def pose_step(i, acc):
        left, right = [], []
        for j in range(2):
            t = 2 * i + j
            ids = opose[pl.ds(t, 1), :]
            mask = jnp.broadcast_to(ids >> 7, (8, LANES)) == sub8
            rows = []
            for a in range(6):
                value = jnp.broadcast_to(pull[a, pl.ds(t, 1), :], (8, LANES))
                rows += three_parts(jnp.where(mask, value, 0.0))
            left.append(jnp.concatenate(rows, axis=0).astype(BF16))
            right.append(one_hot(ids & 127))
        return acc + dot_entries(jnp.concatenate(left, axis=1), jnp.concatenate(right, axis=1))

    pose_acc = lax.fori_loop(0, 16, pose_step, jnp.zeros((144, LANES), F32), unroll=2)
    for i in (10, 11, 12):
        loads[i].wait()
    for a in range(6):
        base = 24 * a
        grad_obs = pose_acc[base : base + 8] + pose_acc[base + 8 : base + 16] + pose_acc[base + 16 : base + 24]
        refined[a] = grad_obs - pose[a] - eoff[a]

    half = lax.broadcasted_iota(I32, (8, LANES), 1) >> 6
    shift = jnp.where(half == core, 0, 4)

    def landmark_pair(ks):
        left, right = [], []
        for k in ks:
            ids = recv[k, 7:8, :].astype(I32)
            mask = jnp.broadcast_to(ids >> 7, (8, LANES)) + shift == sub8
            rows = []
            for v in range(3):
                value = jnp.broadcast_to(recv[k, 3 + v : 4 + v, :], (8, LANES))
                rows += three_parts(jnp.where(mask, value, 0.0))
            rows.append(jnp.where(mask, jnp.broadcast_to(recv[k, 6:7, :], (8, LANES)), 0.0))
            left.append(jnp.concatenate(rows, axis=0).astype(BF16))
            right.append(one_hot(ids & 127))
        return dot_entries(jnp.concatenate(left, axis=1), jnp.concatenate(right, axis=1))

    acc = jnp.zeros((80, LANES), F32)
    for i in range(CHIPS // 2):
        for k in (2 * i, 2 * i + 1):
            if k:
                exchange(k).wait_recv()
        acc = acc + landmark_pair((2 * i, 2 * i + 1))
    for v in range(3):
        base = 24 * v
        totals[v] = acc[base : base + 8] + acc[base + 8 : base + 16] + acc[base + 16 : base + 24]
    totals[3] = acc[72:80]
    totals_copy = pltpu.make_async_remote_copy(
        src_ref=totals,
        dst_ref=other_totals,
        send_sem=d2d_send.at[1],
        recv_sem=d2d_recv.at[1],
        device_id=partner,
        device_id_type=MESH,
    )
    totals_copy.start()
    cold_copy.wait_recv()
    totals_copy.wait_recv()

    def swapped(q):
        return jnp.concatenate([other_totals[q, 4:8, :], other_totals[q, 0:4, :]], axis=0)

    seen = totals[3] + swapped(3)
    estimate = []
    dual_part = jnp.zeros((8, LANES), F32)
    for v in range(3):
        old = jnp.concatenate([cold[v], other_cold[v]], axis=0)
        new = (old + totals[v] + swapped(v)) / (1.0 + seen)
        estimate.append(new)
        cons[v] = new[0:4]
        change = new - old
        dual_part = dual_part + jnp.where(sub8 < 4, seen * change * change, 0.0)
    cons_out = pltpu.make_async_copy(cons, cons_h, out_sem.at[0])
    cons_out.start()

    def give_back(k):
        peer = at_offset(k, -1)
        return pltpu.make_async_remote_copy(
            src_ref=returning.at[k],
            dst_ref=back.at[chip],
            send_sem=ret_send,
            recv_sem=ret_recv,
            device_id={"robot": peer * 2 + core, "sub": sub},
            device_id_type=MESH,
        )

    primal_part = jnp.zeros((8, LANES), F32)
    for b in (3, 2, 1, 0):
        ks = blocks[b]
        ids = recv[ks, 7, :].astype(I32)
        lo, hi = ids & 127, (ids >> 7) + shift
        alive = recv[ks, 6, :]
        for v in range(3):
            value = jnp.zeros((8, LANES), F32)
            for h in range(8):
                value = jnp.where(hi == h, lane_gather(estimate[v][h : h + 1], lo), value)
            returning[ks, v, :] = value
            differ = alive * (recv[ks, v, :] - value)
            primal_part = primal_part + differ * differ
        returning[ks, 3, :] = alive
        for k in range(8 * b + 7, 8 * b - 1, -1):
            if k:
                give_back(k).start()

    part[0:1, :] = jnp.sum(primal_part, axis=0, keepdims=True)
    part[1:2, :] = PENALTY * PENALTY * jnp.sum(dual_part, axis=0, keepdims=True)
    mine = sub * 2 + core
    p1 = [
        pltpu.make_async_remote_copy(
            src_ref=part,
            dst_ref=part1.at[mine],
            send_sem=p1_send,
            recv_sem=p1_recv,
            device_id=group_peer(dc_, ds),
            device_id_type=MESH,
        )
        for dc_, ds in group
    ]
    for copy in p1:
        copy.start()
    part1[mine] = part[...]
    back[chip] = returning[0]

    for copy in y_copies:
        copy.wait_recv()
    edge_lo, edge_hi = edge[...] & 127, edge[...] >> 7

    def gather_poses(h, far):
        new = []
        for a in range(6):
            row = all_poses[lax.div(h, 8), a, pl.ds(lax.rem(h, 8), 1), :]
            new.append(jnp.where(edge_hi == h, lane_gather(row, edge_lo), far[a]))
        return tuple(new)

    far = lax.fori_loop(0, 32, gather_poses, (zero,) * 6, unroll=4)
    grad = [refined[a] + far[a] for a in range(6)]
    for a in range(6):
        refined[a] = pose[a] + sum(inv[6 * a + b] * grad[b] for b in range(6))
    refined_out = pltpu.make_async_copy(refined, refined_h, out_sem.at[1])
    refined_out.start()

    pltpu.make_async_copy(part1.at[pl.ds(0, 7)], part1.at[pl.ds(0, 7)], p1_recv).wait()
    summed = part1[0]
    for i in range(1, 8):
        summed = summed + part1[i]
    part2[chip] = summed
    p2 = [
        pltpu.make_async_remote_copy(
            src_ref=part2.at[chip],
            dst_ref=part2.at[chip],
            send_sem=p2_send,
            recv_sem=p2_recv,
            device_id={"robot": at_offset(k) * 2 + core, "sub": sub},
            device_id_type=MESH,
        )
        for k in range(CHIPS - 1, 0, -1)
    ]
    for copy in p2:
        copy.start()

    pltpu.make_async_copy(back.at[pl.ds(0, CHIPS - 1)], back.at[pl.ds(0, CHIPS - 1)], ret_recv).wait()
    for b in blocks:
        alive = send[b, 6, :]
        for v in range(3):
            dual[v, b, :] = dc[v, b, :] + alive * (lc[v, b, :] - back[b, v, :])
    dual_out = pltpu.make_async_copy(dual, dual_h, out_sem.at[2])
    dual_out.start()

    pltpu.make_async_copy(part2.at[pl.ds(0, CHIPS - 1)], part2.at[pl.ds(0, CHIPS - 1)], p2_recv).wait()
    total = part2[0]
    for i in range(1, CHIPS):
        total = total + part2[i]
    total = jnp.sum(total, axis=1, keepdims=True)
    norms = jnp.sqrt(total / LANDMARKS)
    norms_ref[...] = jnp.broadcast_to(norms, (2, LANES))

    pltpu.make_async_copy(send.at[pl.ds(0, CHIPS - 1)], send.at[pl.ds(0, CHIPS - 1)], send_sem).wait()
    pltpu.make_async_copy(returning.at[pl.ds(0, CHIPS - 1)], returning.at[pl.ds(0, CHIPS - 1)], ret_send).wait()
    pltpu.make_async_copy(part1.at[pl.ds(0, 7)], part1.at[pl.ds(0, 7)], p1_send).wait()
    pltpu.make_async_copy(part2.at[pl.ds(0, CHIPS - 1)], part2.at[pl.ds(0, CHIPS - 1)], p2_send).wait()
    for copy in y_copies:
        copy.wait_send()
    cold_copy.wait_send()
    totals_copy.wait_send()
    cons_out.wait()
    refined_out.wait()
    dual_out.wait()


SHAPES = [
    ((3, 32, 128), F32), ((3, 32, 128), F32), ((32, 128), I32), ((1, 64), I32), ((3, 4, 128), F32), ((6, 8, 128), F32),
    ((36, 8, 128), F32), ((18, 32, 128), F32), ((3, 32, 128), F32), ((32, 128), I32), ((32, 128), I32), ((8, 128), I32),
    ((6, 8, 128), F32),
]


def body(*args):
    given = [a.reshape(shape) for a, (shape, _) in zip(args, SHAPES, strict=True)]
    anywhere = pl.BlockSpec(memory_space=pl.ANY)
    dma, vmem = pltpu.SemaphoreType.DMA, pltpu.VMEM
    refined, cons, dual, norms = pl.pallas_call(
        kernel,
        out_shape=(
            jax.ShapeDtypeStruct((6, 8, 128), F32),
            jax.ShapeDtypeStruct((3, 4, 128), F32),
            jax.ShapeDtypeStruct((3, 32, 128), F32),
            jax.ShapeDtypeStruct((2, 128), F32),
        ),
        in_specs=[anywhere] * 13,
        out_specs=(anywhere, anywhere, anywhere, pl.BlockSpec(memory_space=vmem)),
        scratch_shapes=[
            *[vmem(shape, dtype) for shape, dtype in SHAPES],
            vmem((CHIPS, 8, LANES), F32),
            vmem((CHIPS, 8, LANES), F32),
            vmem((6, 32, LANES), F32),
            vmem((4, 8, LANES), F32),
            vmem((4, 8, LANES), F32),
            vmem((3, 4, LANES), F32),
            vmem((SUBS, 6, 8, LANES), F32),
            vmem((CHIPS, 4, LANES), F32),
            vmem((CHIPS, 4, LANES), F32),
            vmem((2, LANES), F32),
            vmem((8, 2, LANES), F32),
            vmem((CHIPS, 2, LANES), F32),
            vmem((6, 8, LANES), F32),
            vmem((3, 4, LANES), F32),
            vmem((3, 32, LANES), F32),
            dma((13,)), dma, dma((CHIPS,)), dma((3,)), dma((3,)), dma((2,)), dma((2,)), dma, dma, dma, dma, dma, dma,
            dma((3,)),
        ],
        compiler_params=pltpu.CompilerParams(collective_id=0, has_side_effects=True),
    )(*given)
    return (
        refined.reshape(1, 1, 6, 1024),
        cons.reshape(1, 1, 3, 512),
        dual.reshape(1, 1, 3, 4096),
        norms[:, 0],
    )


def solution(mesh):
    three, four = P("robot", "sub", None), P("robot", "sub", None, None)
    return jax.shard_map(
        body,
        mesh=mesh,
        in_specs=(four, four, three, three, four, four, four, four, four, three, three, three, four),
        out_specs=(four, four, four, P()),
        check_vma=False,
    )
```

time: 215 us -> 35.2 us (0.16)
  other arithmetic: 66.6 us -> 0 us
  local copies, waits for them, and re-layouts: 59.9 us -> 3.9 us
  starting transfers between devices: 39.2 us -> 0 us
  blocking collectives: 35.7 us -> 0 us
  Pallas kernels: 0 us -> 30.5 us
  waiting for transfers between devices: 10.5 us -> 0 us
    scatter-add x2 -> x0, other arithmetic: 45.8 us -> none  [the longest x1 22.9 us: body(): jax.ops.segment_sum(entries, owner_ids, num_segments=owned)]
    all_to_all x4 -> x0, starting transfers between devices: 39.2 us -> none  [the longest x1 13 us: body(): lax.all_to_all(slot_ids, ROBOT, split_axis=1, concat_axis=1, tiled=True)]
    psum x4 -> x0, blocking collectives: 35.7 us -> none  [over_axes(): x = lax.psum(x, axis)]
    gather x3 -> x0, local copies, waits for them, and re-layouts: 32.6 us -> none  [the longest x1 14.1 us: body(): copies_at = copies[:, obs_slot[0, 0]]]
    pallas_call x0 -> x1, Pallas kernels: none -> 30.5 us  [body(): pl.pallas_call(kernel, out_shape=(jax.ShapeDtypeStruct((6, 8, 128), F32),...]
    all_to_all x4 -> x0, waiting for transfers between devices: 10.5 us -> none  [the longest x1 7.81 us: body(): lax.all_to_all(returning, ROBOT, split_axis=1, concat_axis=1, tiled=True)]
    all_to_all x9 -> x0, local copies, waits for them, and re-layouts: 7.76 us -> none  [the longest x4 4.43 us: body(): lax.all_to_all(returning, ROBOT, split_axis=1, concat_axis=1, tiled=True)]
    unnamed x34 -> x7, local copies, waits for them, and re-layouts: 9.16 us -> 2.58 us
  transfers between devices with their start and end apart: 4 -> 0, of which waited for: 2 -> 0; matrix products, arithmetic and copies ran while one was open for 33% -> 0% of each run, Pallas kernels for 0% -> 0%
where the time goes in v1:
time: 35.2 us; the launch traced here: 35 us
  Pallas kernels  30.5 us (87%)
  local copies, waits for them, and re-layouts  3.9 us (11%)
  between operations  0.66 us (2%)
    pallas_call x1, Pallas kernels, body(): pl.pallas_call(kernel, out_shape=(jax.ShapeDtypeStruct((6, 8, 128), F32),...  30.5 us
    unnamed x7, local copies, waits for them, and re-layouts  2.58 us
    slice x1, local copies, waits for them, and re-layouts, body(): norms[:, 0]  1.32 us

profile of v1, /device:TPU:1, one launch (start us, length us, event | category | flops | bytes accessed | tf_op | source)
XLA Modules:
  0.0 35.0 jit_solution(2237226125575032507)
XLA Ops:
  0.6 30.5 %shard_map.156 = (f32[6,8,128]{2,1,0:T(8,128)}, f32[3,4,128]{2,1,0:T(4,128)}, f32[3,32,128]{2,1,0:T(8,128)}, f32[2,128]{1,0:T(2,128)}) custom-call(f32[3,32,128]{2,1,0:T(8,128)} %bitcast.18, f32[3,32,128]{2,1,0:T(8,128)} %bitcast.19, s32[32,128]{1,0:T(8,128)} %bitcast.25, s32[1,64]{1,0:T(1,128)} %bitcast.31, f32[3,4,128]{2,1,0:T(4,128)} %bitcast.28, ...), custom_call_target="tpu_custom_call" | custom-call | tf_op jit(solution)/shard_map/pallas_call | solution.py:381
  31.1 0.0 copy-start
  31.1 1.3 %slice_reduce_fusion = f32[2]{0:T(128)} fusion(f32[2,128]{1,0:T(2,128)} %get-tuple-element.11), kind=kLoop, calls=%fused_computation | loop fusion | bytes 16 | tf_op jit(solution)/shard_map/slice | solution.py:417
  32.4 0.0 copy-start.1
  32.4 1.4 %copy.26 = f32[1,1,6,1024]{3,1,2,0:T(1,128)} copy(f32[1,1,6,1024]{3,1,2,0:T(1,128)} %bitcast.24) | data formatting | bytes 49152
  33.8 0.0 copy-done.1
  33.8 0.6 %copy.27 = f32[1,1,3,512]{3,1,2,0:T(1,128)} copy(f32[1,1,3,512]{3,1,2,0:T(1,128)S(1)} %bitcast.29) | data formatting | bytes 12288
  34.4 0.0 copy-done
  34.4 0.6 %copy.28 = f32[1,1,3,4096]{3,1,2,0:T(1,128)} copy(f32[1,1,3,4096]{3,1,2,0:T(1,128)S(1)} %bitcast.21) | data formatting | bytes 98304
Async XLA Ops:
  31.1 3.3 %copy-start = (f32[3,32,128]{2,1,0:T(8,128)S(1)}, f32[3,32,128]{2,1,0:T(8,128)}, u32[]{:S(2)}) copy-start(f32[3,32,128]{2,1,0:T(8,128)} %get-tuple-element.10) | copy-start | bytes 147460
  32.4 1.4 %copy-start.1 = (f32[3,4,128]{2,1,0:T(4,128)S(1)}, f32[3,4,128]{2,1,0:T(4,128)}, u32[]{:S(2)}) copy-start(f32[3,4,128]{2,1,0:T(4,128)} %get-tuple-element.9) | copy-start | bytes 18436

commit v2 on v1

--- a/solution.py
+++ b/solution.py
@@ -45,16 +45,42 @@
 
 def kernel(
     lc_h, dc_h, vis_h, cnt_h, cold_h, pose_h, inv_h, jac_h, meas_h, opose_h, oslot_h, edge_h, eoff_h,
-    refined_h, cons_h, dual_h, norms_ref,
+    refined, cons, dual, norms_ref,
     lc, dc, vis, cnt, cold, pose, inv, jac, meas, opose, oslot, edge, eoff,
     send, recv, pull, totals, other_totals, other_cold, all_poses, returning, back, part, part1, part2,
-    refined, cons, dual,
     load_sem, send_sem, recv_sem, y_send, y_recv, d2d_send, d2d_recv, ret_send, ret_recv,
-    p1_send, p1_recv, p2_send, p2_recv, out_sem,
+    p1_send, p1_recv, p2_send, p2_recv,
 ):
     robot, sub = lax.axis_index("robot"), lax.axis_index("sub")
     core, chip = lax.rem(robot, 2), lax.div(robot, 2)
     x, z = lax.div(chip, NZ), lax.rem(chip, NZ)
+
+    def at_offset(k, sign=1):
+        dx, dz = OFFSETS[k]
+        px = lax.rem(x + (dx if sign > 0 else NX - dx), NX)
+        pz = lax.rem(z + (dz if sign > 0 else NZ - dz), NZ)
+        return px * NZ + pz
+
+    group = [(dc_, ds) for dc_ in range(2) for ds in range(SUBS) if (dc_, ds) != (0, 0)]
+
+    def group_peer(dc_, ds):
+        return {
+            "robot": chip * 2 + lax.rem(core + dc_, 2),
+            "sub": lax.rem(sub + ds, SUBS),
+        }
+
+    barrier = pltpu.get_barrier_semaphore()
+    for k in range(CHIPS - 1, 0, -1):
+        pl.semaphore_signal(
+            barrier,
+            inc=1,
+            device_id={"robot": at_offset(k) * 2 + core, "sub": sub},
+            device_id_type=MESH,
+        )
+    for dc_, ds in group:
+        pl.semaphore_signal(
+            barrier, inc=1, device_id=group_peer(dc_, ds), device_id_type=MESH
+        )
 
     loads = [
         pltpu.make_async_copy(src, dst, load_sem.at[i])
@@ -65,33 +91,6 @@
     ]
     for load in loads:
         load.start()
-
-    def at_offset(k, sign=1):
-        dx, dz = OFFSETS[k]
-        px = lax.rem(x + (dx if sign > 0 else NX - dx), NX)
-        pz = lax.rem(z + (dz if sign > 0 else NZ - dz), NZ)
-        return px * NZ + pz
-
-    group = [(dc_, ds) for dc_ in range(2) for ds in range(SUBS) if (dc_, ds) != (0, 0)]
-
-    def group_peer(dc_, ds):
-        return {
-            "robot": chip * 2 + lax.rem(core + dc_, 2),
-            "sub": lax.rem(sub + ds, SUBS),
-        }
-
-    barrier = pltpu.get_barrier_semaphore()
-    for k in range(1, CHIPS):
-        pl.semaphore_signal(
-            barrier,
-            inc=1,
-            device_id={"robot": at_offset(k) * 2 + core, "sub": sub},
-            device_id_type=MESH,
-        )
-    for dc_, ds in group:
-        pl.semaphore_signal(
-            barrier, inc=1, device_id=group_peer(dc_, ds), device_id_type=MESH
-        )
 
     for i in range(4):
         loads[i].wait()
@@ -113,6 +112,28 @@
     all_poses[sub] = pose[...]
     loads[5].wait()
 
+    loads[6].wait()
+    blocks = [slice(8 * b, 8 * b + 8) for b in range(4)]
+    slot_lo = [oslot[b, :] & 127 for b in blocks]
+    slot_hi = [oslot[b, :] >> 7 for b in blocks]
+
+    def gather_copies(h, found):
+        new = []
+        for v in range(3):
+            row = lc[v, pl.ds(h, 1), :]
+            for b in range(4):
+                new.append(jnp.where(slot_hi[b] == h, lane_gather(row, slot_lo[b]), found[4 * v + b]))
+        return tuple(new)
+
+    zero = jnp.zeros((8, LANES), F32)
+    found = lax.fori_loop(0, 32, gather_copies, (zero,) * 12, unroll=4)
+    for i in (7, 8, 9):
+        loads[i].wait()
+    for b in range(4):
+        error = [meas[v, blocks[b], :] - found[4 * v + b] for v in range(3)]
+        for a in range(6):
+            pull[a, blocks[b], :] = sum(jac[6 * k + a, blocks[b], :] * error[k] for k in range(3))
+
     pl.semaphore_wait(barrier, CHIPS - 1 + len(group))
 
     def exchange(k):
@@ -151,28 +172,6 @@
         device_id_type=MESH,
     )
     cold_copy.start()
-
-    loads[6].wait()
-    blocks = [slice(8 * b, 8 * b + 8) for b in range(4)]
-    slot_lo = [oslot[b, :] & 127 for b in blocks]
-    slot_hi = [oslot[b, :] >> 7 for b in blocks]
-
-    def gather_copies(h, found):
-        new = []
-        for v in range(3):
-            row = lc[v, pl.ds(h, 1), :]
-            for b in range(4):
-                new.append(jnp.where(slot_hi[b] == h, lane_gather(row, slot_lo[b]), found[4 * v + b]))
-        return tuple(new)
-
-    zero = jnp.zeros((8, LANES), F32)
-    found = lax.fori_loop(0, 32, gather_copies, (zero,) * 12, unroll=4)
-    for i in (7, 8, 9):
-        loads[i].wait()
-    for b in range(4):
-        error = [meas[v, blocks[b], :] - found[4 * v + b] for v in range(3)]
-        for a in range(6):
-            pull[a, blocks[b], :] = sum(jac[6 * k + a, blocks[b], :] * error[k] for k in range(3))
 
     sub8 = lax.broadcasted_iota(I32, (8, LANES), 0)
 
@@ -250,9 +249,6 @@
         cons[v] = new[0:4]
         change = new - old
         dual_part = dual_part + jnp.where(sub8 < 4, seen * change * change, 0.0)
-    cons_out = pltpu.make_async_copy(cons, cons_h, out_sem.at[0])
-    cons_out.start()
-
     def give_back(k):
         peer = at_offset(k, -1)
         return pltpu.make_async_remote_copy(
@@ -316,8 +312,6 @@
     grad = [refined[a] + far[a] for a in range(6)]
     for a in range(6):
         refined[a] = pose[a] + sum(inv[6 * a + b] * grad[b] for b in range(6))
-    refined_out = pltpu.make_async_copy(refined, refined_h, out_sem.at[1])
-    refined_out.start()
 
     pltpu.make_async_copy(part1.at[pl.ds(0, 7)], part1.at[pl.ds(0, 7)], p1_recv).wait()
     summed = part1[0]
@@ -343,16 +337,14 @@
         alive = send[b, 6, :]
         for v in range(3):
             dual[v, b, :] = dc[v, b, :] + alive * (lc[v, b, :] - back[b, v, :])
-    dual_out = pltpu.make_async_copy(dual, dual_h, out_sem.at[2])
-    dual_out.start()
 
     pltpu.make_async_copy(part2.at[pl.ds(0, CHIPS - 1)], part2.at[pl.ds(0, CHIPS - 1)], p2_recv).wait()
     total = part2[0]
     for i in range(1, CHIPS):
         total = total + part2[i]
     total = jnp.sum(total, axis=1, keepdims=True)
-    norms = jnp.sqrt(total / LANDMARKS)
-    norms_ref[...] = jnp.broadcast_to(norms, (2, LANES))
+    norms = jnp.broadcast_to(jnp.sqrt(total / LANDMARKS), (2, LANES))
+    norms_ref[...] = jnp.where(lax.broadcasted_iota(I32, (1, LANES), 1) == 0, norms[0:1], norms[1:2])
 
     pltpu.make_async_copy(send.at[pl.ds(0, CHIPS - 1)], send.at[pl.ds(0, CHIPS - 1)], send_sem).wait()
     pltpu.make_async_copy(returning.at[pl.ds(0, CHIPS - 1)], returning.at[pl.ds(0, CHIPS - 1)], ret_send).wait()
@@ -362,9 +354,6 @@
         copy.wait_send()
     cold_copy.wait_send()
     totals_copy.wait_send()
-    cons_out.wait()
-    refined_out.wait()
-    dual_out.wait()
 
 
 SHAPES = [
@@ -373,21 +362,30 @@
     ((6, 8, 128), F32),
 ]
 
+OUT_SHAPES = [(6, 8, 128), (3, 4, 128), (3, 32, 128), (1, 128)]
+
+
+def write_out(refined, cons, dual, norms, refined_h, cons_h, dual_h, norms_out, sem):
+    copies = [
+        pltpu.make_async_copy(src, dst, sem.at[i])
+        for i, (src, dst) in enumerate([(dual, dual_h), (refined, refined_h), (cons, cons_h)])
+    ]
+    for copy in copies:
+        copy.start()
+    norms_out[...] = norms[:, 0:2]
+    for copy in copies:
+        copy.wait()
+
 
 def body(*args):
     given = [a.reshape(shape) for a, (shape, _) in zip(args, SHAPES, strict=True)]
     anywhere = pl.BlockSpec(memory_space=pl.ANY)
     dma, vmem = pltpu.SemaphoreType.DMA, pltpu.VMEM
-    refined, cons, dual, norms = pl.pallas_call(
+    results = pl.pallas_call(
         kernel,
-        out_shape=(
-            jax.ShapeDtypeStruct((6, 8, 128), F32),
-            jax.ShapeDtypeStruct((3, 4, 128), F32),
-            jax.ShapeDtypeStruct((3, 32, 128), F32),
-            jax.ShapeDtypeStruct((2, 128), F32),
-        ),
+        out_shape=tuple(vmem(shape, F32) for shape in OUT_SHAPES),
         in_specs=[anywhere] * 13,
-        out_specs=(anywhere, anywhere, anywhere, pl.BlockSpec(memory_space=vmem)),
+        out_specs=(pl.BlockSpec(memory_space=vmem),) * 4,
         scratch_shapes=[
             *[vmem(shape, dtype) for shape, dtype in SHAPES],
             vmem((CHIPS, 8, LANES), F32),
@@ -402,19 +400,22 @@
             vmem((2, LANES), F32),
             vmem((8, 2, LANES), F32),
             vmem((CHIPS, 2, LANES), F32),
-            vmem((6, 8, LANES), F32),
-            vmem((3, 4, LANES), F32),
-            vmem((3, 32, LANES), F32),
             dma((13,)), dma, dma((CHIPS,)), dma((3,)), dma((3,)), dma((2,)), dma((2,)), dma, dma, dma, dma, dma, dma,
-            dma((3,)),
         ],
         compiler_params=pltpu.CompilerParams(collective_id=0, has_side_effects=True),
     )(*given)
+    refined, cons, dual, norms = pl.pallas_call(
+        write_out,
+        out_shape=tuple(jax.ShapeDtypeStruct(shape, F32) for shape in OUT_SHAPES[:3] + [(1, 2)]),
+        in_specs=[pl.BlockSpec(memory_space=vmem)] * 4,
+        out_specs=(anywhere, anywhere, anywhere, pl.BlockSpec(memory_space=vmem)),
+        scratch_shapes=[dma((3,))],
+    )(*[pltpu.with_memory_space_constraint(r, vmem) for r in results])
     return (
         refined.reshape(1, 1, 6, 1024),
         cons.reshape(1, 1, 3, 512),
         dual.reshape(1, 1, 3, 4096),
-        norms[:, 0],
+        norms.reshape(2),
     )
 
 

time: 35.2 us -> 31.4 us (0.89)
  local copies, waits for them, and re-layouts: 3.9 us -> 0 us
    unnamed x7 -> x0, local copies, waits for them, and re-layouts: 2.58 us -> none
    slice x1 -> x0, local copies, waits for them, and re-layouts: 1.32 us -> none  [body(): norms[:, 0]]
    pallas_call x1 -> x2, Pallas kernels: 30.5 us -> 30.7 us  [the longest x1 29.5 us: body(): pl.pallas_call(kernel, out_shape=tuple((vmem(shape, F32) for shape in OUT...]
where the time goes in v2:
time: 31.4 us; the launch traced here: 31.3 us
  Pallas kernels  30.7 us (98%)
  between operations  0.64 us (2%)
    pallas_call x1, Pallas kernels, body(): pl.pallas_call(kernel, out_shape=tuple((vmem(shape, F32) for shape in OUT...  29.5 us
    pallas_call x1, Pallas kernels, body(): pl.pallas_call(write_out, out_shape=tuple((jax.ShapeDtypeStruct(shape, F3...  1.16 us

profile of v2, /device:TPU:1, one launch (start us, length us, event | category | flops | bytes accessed | tf_op | source)
XLA Modules:
  0.0 31.3 jit_solution(9407489289036070497)
XLA Ops:
  0.6 29.5 %shard_map.156 = (f32[6,8,128]{2,1,0:T(8,128)S(1)}, f32[3,4,128]{2,1,0:T(4,128)S(1)}, f32[3,32,128]{2,1,0:T(8,128)S(1)}, f32[1,128]{1,0:T(1,128)S(1)}) custom-call(f32[3,32,128]{2,1,0:T(8,128)} %bitcast.19, f32[3,32,128]{2,1,0:T(8,128)} %bitcast.20, s32[32,128]{1,0:T(8,128)} %bitcast.24, s32[1,64]{1,0:T(1,128)} %bitcast.29, f32[3,4,128]{2,1,0:T(4,128)} %bitcast.27, ...), custom_call_target="tpu_custom_call" | custom-call | tf_op jit(solution)/shard_map/pallas_call | solution.py:384
  30.2 1.2 %shard_map.157 = (f32[6,8,128]{2,1,0:T(8,128)}, f32[3,4,128]{2,1,0:T(4,128)}, f32[3,32,128]{2,1,0:T(8,128)}, f32[1,2]{1,0:T(1,128)}) custom-call(f32[6,8,128]{2,1,0:T(8,128)S(1)} %get-tuple-element.12.refined, f32[3,4,128]{2,1,0:T(4,128)S(1)} %get-tuple-element.13.cons, f32[3,32,128]{2,1,0:T(8,128)S(1)} %get-tuple-element.14.dual, ...), custom_call_target="tpu_custom_call" | custom-call | tf_op jit(solution)/shard_map/pallas_call | solution.py:407
